TPU v7x, 32 devices: a whole 2x2x4 slice. The times are simulated.
32 devices in a mesh: dp: 4 (over z), tensor: 8 (over y, x, core).
Axes of the slice: x: 2, y: 2, z: 4, core: 2. Of those that a mesh axis runs over, the one named last changes fastest.
Arguments:
- projected: bfloat16 [2, 4096, 4608], P(None, ('dp', 'tensor')), may hold values from -60 to 60
- out_grad: bfloat16 [2, 4096, 4608], P(None, ('dp', 'tensor')), may hold values from -20 to 20
- attention: bfloat16 [2, 4096, 4096], P(None, 'dp', 'tensor'), may hold values from -6 to 6
- w_out: bfloat16 [4096, 4608], P('tensor'), may hold values from -0.09375 to 0.09375
- gains: float32 [4608], replicated, may hold values from 0.5 to 1.5
- main_out: float32 [4096, 4608], P('tensor', 'dp'), may hold values from -6 to 6
- main_gains: float32 [4608], replicated, may hold values from -6 to 6
Outputs:
- attn_grad: bfloat16 [2, 4096, 4096], P(None, 'dp', 'tensor')
- new_main_out: float32 [4096, 4608], P('tensor', 'dp')
- new_main_gains: float32 [4608], replicated
All inputs are finite; a program needn't handle non-finite values.
Results may differ from a plain program's by a relative error of at most 0.0049.
Values may be sent and summed in bfloat16 or wider, within the bound.
A program may use at most 128 MiB of HBM per device.

v0:
```python
import math

import jax
import jax.numpy as jnp
from jax import lax
from jax.sharding import PartitionSpec as P


def normalized(values):
    inverse = lax.rsqrt(jnp.mean(values * values, axis=-1, keepdims=True) + 1e-06)
    return (values * inverse, inverse)


def norm_back(upstream, normed, inverse):
    return inverse * (upstream - normed * jnp.mean(upstream * normed, axis=-1, keepdims=True))


def per_device(projected, out_grad, attention, w_out, gains, main_out, main_gains):
    micro_count = projected.shape[0]
    own_rows = projected.shape[1]
    tokens_all = micro_count * own_rows * lax.axis_size("dp") * lax.axis_size("tensor")
    factor = 1.0 / math.sqrt(tokens_all)
    gain_total = jnp.zeros(gains.shape, jnp.float32)
    back_list = []
    for micro_step in range(micro_count):
        output_in = projected[micro_step].astype(jnp.float32)
        upstream = out_grad[micro_step].astype(jnp.float32)
        out_hat, out_inv = normalized(output_in)
        out_gain = jnp.sum(upstream * out_hat, axis=0)
        out_back = norm_back(upstream * gains, out_hat, out_inv).astype(jnp.bfloat16)
        back_list.append(out_back)
        gain_total = gain_total + lax.psum(out_gain, ("dp", "tensor"))
    stacked = jnp.stack(back_list)
    section = lax.all_gather(stacked, "tensor", axis=1, tiled=True)
    weight_sum = lax.dot_general(
        attention, section, (((0, 1), (0, 1)), ((), ())), preferred_element_type=jnp.float32
    )
    product = lax.dot_general(
        section, w_out, (((2,), (1,)), ((), ())), preferred_element_type=jnp.float32
    ).astype(jnp.bfloat16)
    shard_out = lax.psum_scatter(weight_sum, "dp", scatter_dimension=1, tiled=True)
    return (product, main_out + factor * shard_out, main_gains + factor * gain_total)


def solution(mesh):
    placed = (
        P(None, ("dp", "tensor"), None),
        P(None, ("dp", "tensor"), None),
        P(None, "dp", "tensor"),
        P("tensor", None),
        P(),
        P("tensor", "dp"),
        P(),
    )
    return jax.shard_map(
        per_device,
        mesh=mesh,
        in_specs=placed,
        out_specs=(P(None, "dp", "tensor"), P("tensor", "dp"), P()),
        check_vma=False,
    )
```

profile of v0, /device:TPU:0, one launch (start us, length us, event | category | flops | bytes accessed | tf_op | source)
XLA Modules:
  0.0 310.6 jit_solution(4926830392892736923)
XLA Ops:
  7.2 0.0 copy-start
  7.2 0.0 all-gather.2.cloned.1.call-start
  7.2 0.0 copy-start.1
  7.2 2.3 fusion.22
  9.6 0.2 copy-done.1
  9.7 0.0 copy-start.2
  9.7 0.0 copy-start.3
  9.7 3.5 %fusion.13 = (f32[128]{0:T(128)S(1)}, f32[128]{0:T(128)S(1)}, f32[4608]{0:T(1024)S(1)}, f32[4608]{0:T(1024)S(1)}) fusion(f32[128]{0:T(128)S(1)} %get-tuple-element.15, f32[4608]{0:T(1024)} %param.11, bf16[2,128,4608]{2,1,0:T(8,128)(2,1)} %param.8, bf16[2,128,4608]{2,1,0:T(8,128)(2,1)S(1)} %copy-done.1, f32[128]{0:T(128)S(1)} %get-tuple-element.14), kind=kLoop, calls=%fused_computation.22 | loop fusion | flops 9427712 | bytes 4775936 | tf_op jit(solution)/shard_map/reduce_sum | solution.py:15
  13.2 0.0 copy-done.2
  13.2 0.0 copy-done.3
  13.2 1.4 fusion.17
  14.7 1.6 pad_maximum_fusion
  16.3 0.0 all-gather.2.cloned.1.call-update
  16.3 0.0 reduce-scatter.2.cloned.1.call-start
  16.4 101.4 %all-gather.2.cloned.1.call-done = bf16[2,1024,4608]{2,1,0:T(8,128)(2,1)} async-done(((bf16[2,128,4608]{2,1,0:T(8,128)(2,1)}), bf16[2,1024,4608]{2,1,0:T(8,128)(2,1)}) %all-gather.2.cloned.1.call-update) | async-done | bytes 18874384 | tf_op jit(solution)/shard_map/all_gather | solution.py:34
  117.8 0.0 copy-done
  117.8 16.1 %convolution_bitcast_fusion = f32[512,4608]{0,1:T(8,128)} fusion(bf16[2,1024,4608]{2,1,0:T(8,128)(2,1)} %all-gather.2.cloned.1.call-done, bf16[2,1024,512]{2,1,0:T(8,128)(2,1)S(1)} %copy-done), kind=kOutput, calls=%fused_computation | convolution fusion | flops 9663676416 | bytes 30408704 | tf_op jit(solution)/shard_map/dot_general | solution.py:35
  133.9 0.0 reduce-scatter.2.cloned.1.call-update
  134.0 0.0 copy-start.4
  134.0 3.0 copy.11
  137.0 46.6 %psum.16 = f32[4608]{0:T(1024)S(1)} all-reduce(f32[4608]{0:T(1024)S(1)} %add.34), channel_id=1, replica_groups=mesh['dp'=4,'tensor'=8] {'dp','tensor'}, use_global_device_ids=true, to_apply=%region_6.0 | all-reduce | flops 4608 | bytes 36864 | tf_op jit(solution)/shard_map/psum | solution.py:32
  183.6 0.0 copy-done.4
  183.6 0.6 multiply_add_fusion.1
  184.2 16.2 %fusion.26 = bf16[2,1024,512]{2,1,0:T(8,128)(2,1)} fusion(bf16[2,1024,4608]{2,1,0:T(8,128)(2,1)} %all-gather.2.cloned.1.call-done, bf16[512,4608]{1,0:T(8,128)(2,1)} %param.10), kind=kOutput, calls=%fused_computation.37 | convolution fusion | flops 9664724992 | bytes 25690112 | tf_op jit(solution)/shard_map/dot_general | solution.py:38
  200.4 95.9 %reduce-scatter.2.cloned.1.call-done = f32[512,1152]{0,1:T(8,128)} async-done(((f32[512,4608]{0,1:T(8,128)}), f32[512,1152]{0,1:T(8,128)}) %reduce-scatter.2.cloned.1.call-update) | async-done | bytes 2359312 | tf_op jit(solution)/shard_map/reduce_scatter | solution.py:41
  296.4 4.3 %multiply_add_fusion = f32[512,1152]{0,1:T(8,128)} fusion(f32[512,1152]{0,1:T(8,128)} %copy.11, f32[512,1152]{0,1:T(8,128)} %reduce-scatter.2.cloned.1.call-done), kind=kLoop, calls=%fused_computation.36 | loop fusion | flops 1179648 | bytes 7077888 | tf_op jit(solution)/shard_map/add | solution.py:42
  300.7 3.0 copy.12
  (4 shorter events, 0.0 us)
Async XLA Ops:
  7.2 110.6 %copy-start = (bf16[2,1024,512]{2,1,0:T(8,128)(2,1)S(1)}, bf16[2,1024,512]{2,1,0:T(8,128)(2,1)}, u32[]{:S(2)}) copy-start(bf16[2,1024,512]{2,1,0:T(8,128)(2,1)} %param.9) | copy-start | bytes 6291460
  7.2 110.6 %all-gather.2.cloned.1.call-start = ((), (), s32[]{:S(2)}) async-start(), calls=%async_computation.1 | async-start | bytes 21233664 | tf_op jit(solution)/shard_map/all_gather | solution.py:34
  7.2 2.5 copy-start.1
  9.7 3.5 %copy-start.2 = (bf16[2,128,4608]{2,1,0:T(8,128)(2,1)S(1)}, bf16[2,128,4608]{2,1,0:T(8,128)(2,1)}, u32[]{:S(2)}) copy-start(bf16[2,128,4608]{2,1,0:T(8,128)(2,1)} %param.8) | copy-start | bytes 7077892
  9.7 3.5 %copy-start.3 = (f32[4608]{0:T(1024)S(1)}, f32[4608]{0:T(1024)}, u32[]{:S(2)}) copy-start(f32[4608]{0:T(1024)} %param.11) | copy-start | bytes 55300
  16.3 280.0 %reduce-scatter.2.cloned.1.call-start = ((), (), s32[]{:S(2)}) async-start(), calls=%async_computation.2 | async-start | bytes 11796480 | tf_op jit(solution)/shard_map/reduce_scatter | solution.py:41
  134.0 49.6 %copy-start.4 = (f32[4608]{0:T(1024)S(1)}, f32[4608]{0:T(1024)}, u32[]{:S(2)}) copy-start(f32[4608]{0:T(1024)} %param.13) | copy-start | bytes 55300
Sparse Core Ops, SparseCore 0:
  16.4 101.3 all-gather.1
  134.1 162.2 reduce-scatter.1
where the time goes:
time: 311 us
  waiting for transfers between devices  197 us (63%)
  blocking collectives  46.6 us (15%)
  matrix products  32.4 us (10%)
  between operations  14.1 us (5%)
  other arithmetic  13.8 us (4%)
  local copies, waits for them, and re-layouts  6.29 us (2%)
    all_gather x1, waiting for transfers between devices, per_device(): section = lax.all_gather(stacked, 'tensor', axis=1, tiled=True)  101 us
    reduce_scatter x1, waiting for transfers between devices, per_device(): lax.psum_scatter(weight_sum, 'dp', scatter_dimension=1, tiled=True)  95.9 us
    psum x1, blocking collectives, per_device(): gain_total = gain_total + lax.psum(out_gain, ('dp', 'tensor'))  46.6 us
    dot_general x1, matrix products, per_device(): lax.dot_general(section, w_out, (((2,), (1,)), ((), ())), preferred_eleme...  16.2 us
    dot_general x1, matrix products, per_device(): lax.dot_general(attention, section, (((0, 1), (0, 1)), ((), ())), preferr...  16.1 us
    unnamed x12, local copies, waits for them, and re-layouts  6.29 us
  transfers between devices with their start and end apart: 2, of which 2 were waited for; matrix products, arithmetic and copies ran while one was open for 6% of the time, Pallas kernels for 0%

commit v1 on v0

v1 whole, which is shorter than its diff:
```python
import functools
import math

import jax
import jax.numpy as jnp
from jax import lax
from jax.experimental import pallas as pl
from jax.experimental.pallas import tpu as pltpu
from jax.sharding import PartitionSpec as P

MESH = pl.DeviceIdType.MESH
LANES = 128
TILE = 16


def flip(index, step):
    return index + step * (1 - 2 * (lax.div(index, step) % 2))


def combine(index, steps):
    found = [index]
    for step in steps:
        found = found + [flip(each, step) for each in found]
    return found


def kernel(
    dims,
    proj_hbm, grad_hbm, att_hbm, w_hbm, gains_ref,
    attn_hbm, sum_hbm, gain_hbm,
    own_in, held, w_buf, att_in, att_t, acc, part, arrived, out_sum, gain_acc, gain_mine, gain_got,
    in_sem, w_sem, att_sem, out_sem,
    ag_send, ag_recv, pair_send, pair_recv, rs_send, rs_recv, gain_send, gain_recv,
):
    T, DP, D_true, micro, own, heads, wide, K = dims
    w = LANES
    R = micro * own
    L = (T // 2).bit_length() - 1
    C = T // 2
    t_me = lax.axis_index("tensor")
    d_me = lax.axis_index("dp")
    d_width = wide // DP
    t_pair = flip(t_me, 1)
    chip_steps = [2 << bit for bit in range(L)]
    cuts = [R * i // L // TILE * TILE for i in range(L)] + [R]

    blocks = 8
    height = R // blocks

    def load(block):
        slot = block % 2
        rows = pl.ds(block * height, height)
        return (
            pltpu.make_async_copy(proj_hbm.at[rows], own_in.at[slot, 0], in_sem.at[slot, 0]),
            pltpu.make_async_copy(grad_hbm.at[rows], own_in.at[slot, 1], in_sem.at[slot, 1]),
        )

    for block in range(2):
        for copy in load(block):
            copy.start()

    def att_load(t, slot):
        return [
            pltpu.make_async_copy(
                att_hbm.at[m, pl.ds(t * own, own)], att_in.at[slot, pl.ds(m * own, own)], att_sem.at[slot, m]
            )
            for m in range(micro)
        ]

    for t in range(2):
        for copy in att_load(t, t):
            copy.start()

    def w_load(k, d):
        return pltpu.make_async_copy(
            w_hbm.at[:, pl.ds(pl.multiple_of(d * d_width + k * w, w), w)],
            w_buf.at[k, :, pl.ds(d * w, w)],
            w_sem.at[k, d],
        )

    barrier = pltpu.get_barrier_semaphore()
    partners = [("tensor", t_pair)] + [("tensor", flip(t_me, step)) for step in chip_steps]
    dp_steps = [1 << bit for bit in range(DP.bit_length() - 1)]
    partners += [("dp", flip(d_me, step)) for step in dp_steps]
    for name, where in partners:
        pl.semaphore_signal(barrier, inc=1, device_id={name: where}, device_id_type=MESH)

    @pl.when(d_me > 0)
    def _():
        pl.semaphore_signal(barrier, inc=1, device_id={"dp": d_me - 1}, device_id_type=MESH)

    @pl.when(d_me < DP - 1)
    def _():
        pl.semaphore_signal(barrier, inc=1, device_id={"dp": d_me + 1}, device_id_type=MESH)

    gain_acc[...] = jnp.zeros_like(gain_acc)
    own_base = pl.multiple_of(t_me * R, R)
    for block in range(blocks):
        slot = block % 2
        for copy in load(block):
            copy.wait()

        def rows_step(i, carry, slot=slot, block=block):
            rows = pl.ds(pl.multiple_of(i * TILE, TILE), TILE)
            v = own_in[slot, 0, rows, :].astype(jnp.float32)
            g = own_in[slot, 1, rows, :].astype(jnp.float32)
            u = g * gains_ref[...]
            r = lax.rsqrt(jnp.sum(v * v, axis=-1, keepdims=True) * (1.0 / D_true) + 1e-6)
            n = v * r
            m = jnp.sum(u * n, axis=-1, keepdims=True) * (1.0 / D_true)
            gn = g * n
            gain_acc[...] += gn[:8] + gn[8:]
            back = (r * (u - n * m)).astype(jnp.bfloat16)
            at = pl.ds(pl.multiple_of(own_base + block * height + i * TILE, TILE), TILE)
            for k in range(K):
                for d in range(DP):
                    c0 = d * d_width + k * w
                    held[k, at, d * w:(d + 1) * w] = back[:, c0:c0 + w]
            return carry

        lax.fori_loop(0, height // TILE, rows_step, 0)
        if block + 2 < blocks:
            for copy in load(block + 2):
                copy.start()
    gain_mine[0] = jnp.sum(gain_acc[...], axis=0, keepdims=True)

    waits = len(partners) + jnp.where(d_me > 0, 1, 0) + jnp.where(d_me < DP - 1, 1, 0)
    pl.semaphore_wait(barrier, waits)

    def block_of(k, t, p):
        if p is None:
            return held.at[k, pl.ds(pl.multiple_of(t * R, R), R)]
        return held.at[k, pl.ds(pl.multiple_of(t * R + cuts[p], TILE), cuts[p + 1] - cuts[p])]

    def stage_copies(k, s, receive):
        copies = []
        for p in range(L):
            bits = [chip_steps[(p + i) % L] for i in range(s + 1)]
            peer = flip(t_me, bits[s])
            first = peer if receive else t_me
            for j, src in enumerate(combine(first, bits[:s])):
                index = p * (C - 1) + (1 << s) - 1 + j
                ref = block_of(k, src, p)
                copies.append((p, index, src, pltpu.make_async_remote_copy(
                    src_ref=ref, dst_ref=ref, send_sem=ag_send.at[k, index], recv_sem=ag_recv.at[k, index],
                    device_id={"tensor": peer}, device_id_type=MESH)))
        return copies

    def pair_copy(k, index, src, p):
        ref = block_of(k, src, p)
        return pltpu.make_async_remote_copy(
            src_ref=ref, dst_ref=ref, send_sem=pair_send.at[k, index], recv_sem=pair_recv.at[k, index],
            device_id={"tensor": t_pair}, device_id_type=MESH)

    own_index = L * (C - 1)

    def advance(k, s):
        if s > 0:
            for p, index, src, copy in stage_copies(k, s - 1, True):
                copy.wait_recv()
                if s == L:
                    pair_copy(k, index, src, p).start()
        if s < L:
            for _, _, _, copy in stage_copies(k, s, False):
                copy.start()
            if s > 0:
                for p, index, src, _ in stage_copies(k, s - 1, True):
                    pair_copy(k, index, src, p).start()
            else:
                pair_copy(k, own_index, t_me, None).start()

    def all_received_from_pair(k):
        for s in range(L):
            for p, index, src, _ in stage_copies(k, s, True):
                pair_copy(k, index, flip(src, 1), p).wait_recv()
        pair_copy(k, own_index, t_pair, None).wait_recv()

    def all_sent(k):
        for s in range(L):
            for _, _, _, copy in stage_copies(k, s, False):
                copy.wait_send()
            for p, index, src, _ in stage_copies(k, s, True):
                pair_copy(k, index, src, p).wait_send()
        pair_copy(k, own_index, t_me, None).wait_send()

    def start_w(k, carry):
        for d in range(DP):
            w_load(k, d).start()
        return carry

    def rs_copy(k, d, to_left):
        if to_left:
            slot = jnp.where(d_me - 1 == d, DP, d)
            peer = d_me - 1
        else:
            slot, peer = d, d_me + 1
        return pltpu.make_async_remote_copy(
            src_ref=arrived.at[k, d], dst_ref=arrived.at[k, slot], send_sem=rs_send.at[k, d],
            recv_sem=rs_recv.at[k, slot], device_id={"dp": peer}, device_id_type=MESH)

    def rs_arrival(k, slot):
        return pltpu.make_async_remote_copy(
            src_ref=arrived.at[k, slot], dst_ref=arrived.at[k, slot], send_sem=rs_send.at[k, 0],
            recv_sem=rs_recv.at[k, slot], device_id={"dp": flip(d_me, 1)}, device_id_type=MESH)

    gain_steps = [("tensor", 1)] + [("tensor", s) for s in chip_steps] + [("dp", s) for s in dp_steps]
    S = len(gain_steps)

    def gain_copy(s):
        name, step = gain_steps[s]
        return pltpu.make_async_remote_copy(
            src_ref=gain_mine.at[s], dst_ref=gain_got.at[s], send_sem=gain_send.at[s], recv_sem=gain_recv.at[s],
            device_id={name: flip(t_me if name == "tensor" else d_me, step)}, device_id_type=MESH)

    def within(k):
        return jnp.logical_and(k >= 0, k < K)

    for q in range(min(L, K)):
        advance(q, 0)
    lax.fori_loop(0, K, start_w, 0)

    def turn(t, carry):
        slot = t % 2
        for copy in att_load(t, slot):
            copy.wait()
        att_t[:, pl.ds(pl.multiple_of(t * R, R), R)] = att_in[slot].astype(jnp.float32).T.astype(jnp.bfloat16)

        @pl.when(t + 2 < T)
        def _():
            for copy in att_load(t + 2, slot):
                copy.start()
        return carry

    lax.fori_loop(0, T, turn, 0)

    big = 2 * R
    tiles = T * R // big

    def step(i, carry):
        c = i - (L - 1)
        for s in range(L + 1):
            q = c + L - s

            @pl.when(jnp.logical_and(within(q), jnp.logical_or(q >= L, s > 0)))
            def _(q=q, s=s):
                advance(q, s)

        @pl.when(within(c))
        def _():
            all_received_from_pair(c)
            part[c % DP] = jnp.dot(att_t[...], held[c], preferred_element_type=jnp.float32)

        right = c - d_me
        left = c - (DP - 1 - d_me)
        final = jnp.minimum(left, right)

        def pass_on(k, d, to_left, has_arrival):
            piece = part[k % DP, :, d * w:(d + 1) * w]

            @pl.when(has_arrival)
            def _():
                rs_arrival(k, d).wait_recv()
                arrived[k, d] = (piece + arrived[k, d].astype(jnp.float32)).astype(jnp.bfloat16)

            @pl.when(jnp.logical_not(has_arrival))
            def _():
                arrived[k, d] = piece.astype(jnp.bfloat16)

            rs_copy(k, d, to_left).start()

        for d in reversed(range(1, DP)):
            @pl.when(jnp.logical_and(within(right), d_me < d))
            def _(d=d):
                pass_on(right, d, False, d_me > 0)
        for d in range(DP - 1):
            @pl.when(jnp.logical_and(within(left), d_me > d))
            def _(d=d):
                pass_on(left, d, True, d_me < DP - 1)

        @pl.when(within(c))
        def _():
            for d in range(DP):
                w_load(c, d).wait()

            def tile(n, carry):
                rows = pl.ds(pl.multiple_of(n * big, big), big)
                product = lax.dot_general(
                    held[c, rows, :], w_buf[c], (((1,), (1,)), ((), ())), preferred_element_type=jnp.float32)

                @pl.when(c == 0)
                def _():
                    acc[rows, :] = product

                @pl.when(c > 0)
                def _():
                    acc[rows, :] += product
                return carry

            lax.fori_loop(0, tiles, tile, 0)
            all_sent(c)

        @pl.when(c == K - 1)
        def _():
            def leave(t, carry):
                rows = pl.ds(pl.multiple_of(t * R, R), R)
                held[0, rows, :heads] = acc[rows, :].astype(jnp.bfloat16)
                for m in range(micro):
                    attn_copy(t, m).start()
                return carry
            lax.fori_loop(0, T, leave, 0)

        @pl.when(within(final))
        def _():
            mine = part[final % DP, :, pl.ds(pl.multiple_of(d_me * w, w), w)]
            at = pl.ds(pl.multiple_of(final * w, w), w)
            out_sum[:, at] = mine

            @pl.when(d_me > 0)
            def _():
                rs_arrival(final, d_me).wait_recv()
                out_sum[:, at] += arrived[final, d_me].astype(jnp.float32)

            @pl.when(d_me < DP - 1)
            def _():
                rs_arrival(final, DP).wait_recv()
                out_sum[:, at] += arrived[final, DP].astype(jnp.float32)

        for s in range(S + 1):
            @pl.when(c == s)
            def _(s=s):
                if s > 0:
                    gain_copy(s - 1).wait()
                    gain_mine[s] = gain_mine[s - 1] + gain_got[s - 1]
                if s < S:
                    gain_copy(s).start()
        return carry

    def attn_copy(t, m):
        return pltpu.make_async_copy(
            held.at[0, pl.ds(pl.multiple_of(t * R + m * own, TILE), own), pl.ds(0, heads)],
            attn_hbm.at[m, pl.ds(pl.multiple_of(t * own, TILE), own)],
            out_sem.at[t, m],
        )

    total = max(K + DP - 1, S + 1)
    lax.fori_loop(0, total + L - 1, step, 0)

    sum_out = pltpu.make_async_copy(out_sum, sum_hbm, in_sem.at[0, 0])
    gain_out = pltpu.make_async_copy(gain_mine.at[S], gain_hbm, in_sem.at[0, 1])
    sum_out.start()
    gain_out.start()

    def drain(k, carry):
        for d in range(DP):
            @pl.when(d != d_me)
            def _(d=d):
                pltpu.make_async_remote_copy(
                    src_ref=arrived.at[k, d], dst_ref=arrived.at[k, d], send_sem=rs_send.at[k, d],
                    recv_sem=rs_recv.at[k, d], device_id={"dp": flip(d_me, 1)}, device_id_type=MESH).wait_send()
        return carry

    lax.fori_loop(0, K, drain, 0)

    def attn_wait(t, carry):
        for m in range(micro):
            attn_copy(t, m).wait()
        return carry

    lax.fori_loop(0, T, attn_wait, 0)
    sum_out.wait()
    gain_out.wait()


def padded(values, parts, axis):
    size = values.shape[axis] // parts
    extra = -size % LANES
    if extra == 0:
        return values
    shape = values.shape
    split = values.reshape(shape[:axis] + (parts, size) + shape[axis + 1:])
    pads = [(0, 0)] * split.ndim
    pads[axis + 1] = (0, extra)
    return jnp.pad(split, pads).reshape(shape[:axis] + (parts * (size + extra),) + shape[axis + 1:])


def unpadded(values, parts, size, axis):
    have = values.shape[axis] // parts
    if have == size:
        return values
    shape = values.shape
    split = values.reshape(shape[:axis] + (parts, have) + shape[axis + 1:])
    split = lax.slice_in_dim(split, 0, size, axis=axis + 1)
    return split.reshape(shape[:axis] + (parts * size,) + shape[axis + 1:])


def per_device(projected, out_grad, attention, w_out, gains, main_out, main_gains):
    T, DP = lax.axis_size("tensor"), lax.axis_size("dp")
    micro, own, D = projected.shape
    heads = w_out.shape[0]
    piece = D // DP
    factor = 1.0 / math.sqrt(micro * own * DP * T)
    R = micro * own
    proj = padded(projected.reshape(R, D), DP, 1)
    grad = padded(out_grad.reshape(R, D), DP, 1)
    weight = padded(w_out, DP, 1)
    gain_row = padded(gains.reshape(1, D), DP, 1)
    wide = proj.shape[1]
    K = wide // DP // LANES
    C = T // 2
    L = C.bit_length() - 1
    S = 1 + L + DP.bit_length() - 1
    chunk = DP * LANES
    dims = (T, DP, D, micro, own, heads, wide, K)
    count = L * (C - 1)
    DMA = pltpu.SemaphoreType.DMA
    anywhere = pl.BlockSpec(memory_space=pl.ANY)
    attn_grad, total, gain_total = pl.pallas_call(
        functools.partial(kernel, dims),
        out_shape=(
            jax.ShapeDtypeStruct((micro, own * T, heads), jnp.bfloat16),
            jax.ShapeDtypeStruct((heads, wide // DP), jnp.float32),
            jax.ShapeDtypeStruct((1, wide), jnp.float32),
        ),
        in_specs=[anywhere] * 4 + [pl.BlockSpec(memory_space=pltpu.VMEM)],
        out_specs=(anywhere,) * 3,
        scratch_shapes=[
            pltpu.VMEM((2, 2, R // 8, wide), jnp.bfloat16),
            pltpu.VMEM((K, T * R, chunk), jnp.bfloat16),
            pltpu.VMEM((K, heads, chunk), jnp.bfloat16),
            pltpu.VMEM((2, R, heads), jnp.bfloat16),
            pltpu.VMEM((heads, T * R), jnp.bfloat16),
            pltpu.VMEM((T * R, heads), jnp.float32),
            pltpu.VMEM((DP, heads, chunk), jnp.float32),
            pltpu.VMEM((K, DP + 1, heads, LANES), jnp.bfloat16),
            pltpu.VMEM((heads, wide // DP), jnp.float32),
            pltpu.VMEM((8, wide), jnp.float32),
            pltpu.VMEM((S + 1, 1, wide), jnp.float32),
            pltpu.VMEM((S, 1, wide), jnp.float32),
            DMA((2, 2)), DMA((K, DP)), DMA((2, micro)), DMA((T, micro)),
            DMA((K, count)), DMA((K, count)), DMA((K, count + 1)), DMA((K, count + 1)),
            DMA((K, DP)), DMA((K, DP + 1)), DMA((S,)), DMA((S,)),
        ],
        compiler_params=pltpu.CompilerParams(
            collective_id=0, has_side_effects=True, vmem_limit_bytes=67043328
        ),
    )(proj, grad, attention, weight, gain_row)
    total = unpadded(total, 1, piece, 1)
    gain_total = unpadded(gain_total, DP, piece, 1).reshape(D)
    return (attn_grad, main_out + factor * total, main_gains + factor * gain_total)


def solution(mesh):
    placed = (
        P(None, ("dp", "tensor"), None),
        P(None, ("dp", "tensor"), None),
        P(None, "dp", "tensor"),
        P("tensor", None),
        P(),
        P("tensor", "dp"),
        P(),
    )
    return jax.shard_map(
        per_device,
        mesh=mesh,
        in_specs=placed,
        out_specs=(P(None, "dp", "tensor"), P("tensor", "dp"), P()),
        check_vma=False,
    )
```

time: 311 us -> 123 us (0.40)
  waiting for transfers between devices: 197 us -> 0 us
  Pallas kernels: 0 us -> 115 us
  blocking collectives: 46.6 us -> 0 us
  matrix products: 32.4 us -> 0 us
  between operations: 14.1 us -> 0.67 us
  other arithmetic: 13.8 us -> 4.87 us
  local copies, waits for them, and re-layouts: 6.29 us -> 2.68 us
    pallas_call x0 -> x1, Pallas kernels: none -> 115 us  [per_device(): pl.pallas_call(functools.partial(kernel, dims), out_shape=(jax.ShapeDtype...]
    all_gather x1 -> x0, waiting for transfers between devices: 101 us -> none  [per_device(): section = lax.all_gather(stacked, 'tensor', axis=1, tiled=True)]
    reduce_scatter x1 -> x0, waiting for transfers between devices: 95.9 us -> none  [per_device(): lax.psum_scatter(weight_sum, 'dp', scatter_dimension=1, tiled=True)]
    psum x1 -> x0, blocking collectives: 46.6 us -> none  [per_device(): gain_total = gain_total + lax.psum(out_gain, ('dp', 'tensor'))]
    dot_general x2 -> x0, matrix products: 32.4 us -> none  [the longest x1 16.2 us: per_device(): lax.dot_general(section, w_out, (((2,), (1,)), ((), ())), preferred_eleme...]
    reduce_sum x2 -> x0, other arithmetic: 5.78 us -> none  [the longest x1 3.45 us: norm_back(): jnp.mean(upstream * normed, axis=-1, keepdims=True)]
    unnamed x12 -> x7, local copies, waits for them, and re-layouts: 6.29 us -> 1.33 us
  transfers between devices with their start and end apart: 2 -> 0, of which waited for: 2 -> 0; matrix products, arithmetic and copies ran while one was open for 6% -> 0% of each run, Pallas kernels for 0% -> 0%
where the time goes in v1:
time: 123 us
  Pallas kernels  115 us (93%)
  other arithmetic  4.87 us (4%)
  local copies, waits for them, and re-layouts  2.68 us (2%)
    pallas_call x1, Pallas kernels, per_device(): pl.pallas_call(functools.partial(kernel, dims), out_shape=(jax.ShapeDtype...  115 us
    add x1, other arithmetic, per_device(): main_out + factor * total  4.2 us

profile of v1, /device:TPU:0, one launch (start us, length us, event | category | flops | bytes accessed | tf_op | source)
XLA Modules:
  0.0 122.9 jit_solution(10193794399097589719)
XLA Ops:
  0.6 1.3 %reshape.20.gains_ref = f32[1,4608]{1,0:T(1,128)} reshape(f32[4608]{0:T(1024)} %param.11) | data formatting | bytes 36864 | tf_op jit(solution)/shard_map/reshape | solution.py:406
  2.0 114.7 %shard_map.94 = (bf16[2,1024,512]{2,1,0:T(8,128)(2,1)}, f32[512,1152]{1,0:T(8,128)}, f32[1,4608]{1,0:T(1,128)}) custom-call(bf16[256,4608]{1,0:T(8,128)(2,1)} %bitcast.2, bf16[256,4608]{1,0:T(8,128)(2,1)} %bitcast.3, bf16[2,1024,512]{2,1,0:T(8,128)(2,1)} %att_hbm.1, bf16[512,4608]{1,0:T(8,128)(2,1)} %w_hbm.1, f32[1,4608]{1,0:T(1,128)} %reshape.20.gains_ref), custom_call_target="tpu_custom_call" | custom-call | tf_op jit(solution)/shard_map/pallas_call | solution.py:417
  116.6 0.0 copy-start.2
  116.7 0.0 copy-start.1
  116.7 0.0 copy-start
  116.7 4.2 %multiply_add_fusion = f32[512,1152]{1,0:T(8,128)} fusion(f32[512,1152]{1,0:T(8,128)} %param.12, f32[512,1152]{1,0:T(8,128)} %get-tuple-element.7), kind=kLoop, calls=%fused_computation | loop fusion | flops 1179648 | bytes 7077888 | tf_op jit(solution)/shard_map/add | solution.py:449
  120.9 0.0 copy-done.2
  120.9 0.1 multiply_reduce_fusion
  120.9 0.0 copy-done.1
  121.0 0.6 add.7
  121.6 0.0 copy-done
  121.6 1.3 %copy.11 = bf16[2,1024,512]{2,1,0:T(8,128)(2,1)} copy(bf16[2,1024,512]{2,1,0:T(8,128)(2,1)S(1)} %copy-done) | data formatting | bytes 4194304
Async XLA Ops:
  116.6 4.2 %copy-start.2 = (f32[1,4608]{1,0:T(1,128)S(1)}, f32[1,4608]{1,0:T(1,128)}, u32[]{:S(2)}) copy-start(f32[1,4608]{1,0:T(1,128)} %get-tuple-element.8) | copy-start | bytes 55300
  116.7 4.3 %copy-start.1 = (f32[4608]{0:T(1024)S(1)}, f32[4608]{0:T(1024)}, u32[]{:S(2)}) copy-start(f32[4608]{0:T(1024)} %param.13) | copy-start | bytes 55300
  116.7 4.9 %copy-start = (bf16[2,1024,512]{2,1,0:T(8,128)(2,1)S(1)}, bf16[2,1024,512]{2,1,0:T(8,128)(2,1)}, u32[]{:S(2)}) copy-start(bf16[2,1024,512]{2,1,0:T(8,128)(2,1)} %get-tuple-element.12) | copy-start | bytes 6291460

commit v2 on v1

--- a/solution.py
+++ b/solution.py
@@ -26,10 +26,11 @@
 
 def kernel(
     dims,
-    proj_hbm, grad_hbm, att_hbm, w_hbm, gains_ref,
+    factor,
+    proj_hbm, grad_hbm, att_hbm, w_hbm, main_hbm, gains_ref,
     attn_hbm, sum_hbm, gain_hbm,
     own_in, held, w_buf, att_in, att_t, acc, part, arrived, out_sum, gain_acc, gain_mine, gain_got,
-    in_sem, w_sem, att_sem, out_sem,
+    in_sem, w_sem, att_sem, out_sem, main_sem,
     ag_send, ag_recv, pair_send, pair_recv, rs_send, rs_recv, gain_send, gain_recv,
 ):
     T, DP, D_true, micro, own, heads, wide, K = dims
@@ -70,6 +71,7 @@
     for t in range(2):
         for copy in att_load(t, t):
             copy.start()
+    main_in = pltpu.make_async_copy(main_hbm, out_sum, main_sem)
 
     def w_load(k, d):
         return pltpu.make_async_copy(
@@ -104,7 +106,7 @@
             rows = pl.ds(pl.multiple_of(i * TILE, TILE), TILE)
             v = own_in[slot, 0, rows, :].astype(jnp.float32)
             g = own_in[slot, 1, rows, :].astype(jnp.float32)
-            u = g * gains_ref[...]
+            u = g * gains_ref[...].reshape(1, wide)
             r = lax.rsqrt(jnp.sum(v * v, axis=-1, keepdims=True) * (1.0 / D_true) + 1e-6)
             n = v * r
             m = jnp.sum(u * n, axis=-1, keepdims=True) * (1.0 / D_true)
@@ -218,6 +220,7 @@
     for q in range(min(L, K)):
         advance(q, 0)
     lax.fori_loop(0, K, start_w, 0)
+    main_in.start()
 
     def turn(t, carry):
         slot = t % 2
@@ -231,7 +234,10 @@
                 copy.start()
         return carry
 
-    lax.fori_loop(0, T, turn, 0)
+    lax.fori_loop(0, T // 2, turn, 0)
+    advance(0, 1)
+    lax.fori_loop(T // 2, T, turn, 0)
+    main_in.wait()
 
     big = 2 * R
     tiles = T * R // big
@@ -241,7 +247,7 @@
         for s in range(L + 1):
             q = c + L - s
 
-            @pl.when(jnp.logical_and(within(q), jnp.logical_or(q >= L, s > 0)))
+            @pl.when(jnp.logical_and(within(q), q >= (L if s == 0 else 1 if s == 1 else 0)))
             def _(q=q, s=s):
                 advance(q, s)
 
@@ -313,17 +319,17 @@
         def _():
             mine = part[final % DP, :, pl.ds(pl.multiple_of(d_me * w, w), w)]
             at = pl.ds(pl.multiple_of(final * w, w), w)
-            out_sum[:, at] = mine
+            out_sum[:, at] += factor * mine
 
             @pl.when(d_me > 0)
             def _():
                 rs_arrival(final, d_me).wait_recv()
-                out_sum[:, at] += arrived[final, d_me].astype(jnp.float32)
+                out_sum[:, at] += factor * arrived[final, d_me].astype(jnp.float32)
 
             @pl.when(d_me < DP - 1)
             def _():
                 rs_arrival(final, DP).wait_recv()
-                out_sum[:, at] += arrived[final, DP].astype(jnp.float32)
+                out_sum[:, at] += factor * arrived[final, DP].astype(jnp.float32)
 
         for s in range(S + 1):
             @pl.when(c == s)
@@ -403,7 +409,8 @@
     proj = padded(projected.reshape(R, D), DP, 1)
     grad = padded(out_grad.reshape(R, D), DP, 1)
     weight = padded(w_out, DP, 1)
-    gain_row = padded(gains.reshape(1, D), DP, 1)
+    gain_row = padded(gains, DP, 0)
+    main = padded(main_out, 1, 1)
     wide = proj.shape[1]
     K = wide // DP // LANES
     C = T // 2
@@ -415,13 +422,13 @@
     DMA = pltpu.SemaphoreType.DMA
     anywhere = pl.BlockSpec(memory_space=pl.ANY)
     attn_grad, total, gain_total = pl.pallas_call(
-        functools.partial(kernel, dims),
+        functools.partial(kernel, dims, factor),
         out_shape=(
             jax.ShapeDtypeStruct((micro, own * T, heads), jnp.bfloat16),
             jax.ShapeDtypeStruct((heads, wide // DP), jnp.float32),
             jax.ShapeDtypeStruct((1, wide), jnp.float32),
         ),
-        in_specs=[anywhere] * 4 + [pl.BlockSpec(memory_space=pltpu.VMEM)],
+        in_specs=[anywhere] * 5 + [pl.BlockSpec(memory_space=pltpu.VMEM)],
         out_specs=(anywhere,) * 3,
         scratch_shapes=[
             pltpu.VMEM((2, 2, R // 8, wide), jnp.bfloat16),
@@ -436,17 +443,17 @@
             pltpu.VMEM((8, wide), jnp.float32),
             pltpu.VMEM((S + 1, 1, wide), jnp.float32),
             pltpu.VMEM((S, 1, wide), jnp.float32),
-            DMA((2, 2)), DMA((K, DP)), DMA((2, micro)), DMA((T, micro)),
+            DMA((2, 2)), DMA((K, DP)), DMA((2, micro)), DMA((T, micro)), DMA,
             DMA((K, count)), DMA((K, count)), DMA((K, count + 1)), DMA((K, count + 1)),
             DMA((K, DP)), DMA((K, DP + 1)), DMA((S,)), DMA((S,)),
         ],
         compiler_params=pltpu.CompilerParams(
             collective_id=0, has_side_effects=True, vmem_limit_bytes=67043328
         ),
-    )(proj, grad, attention, weight, gain_row)
+    )(proj, grad, attention, weight, main, gain_row)
     total = unpadded(total, 1, piece, 1)
     gain_total = unpadded(gain_total, DP, piece, 1).reshape(D)
-    return (attn_grad, main_out + factor * total, main_gains + factor * gain_total)
+    return (attn_grad, total, main_gains + factor * gain_total)
 
 
 def solution(mesh):

time: 123 us -> 122 us (level)
  other arithmetic: 4.87 us -> 2.26 us
  local copies, waits for them, and re-layouts: 2.68 us -> 4.45 us
    add x2 -> x1, other arithmetic: 4.81 us -> 1.34 us  [per_device(): return (attn_grad, total, main_gains + factor * gain_total)]
    unnamed x7 -> x4, local copies, waits for them, and re-layouts: 1.33 us -> 4.45 us
    reshape x1 -> x0, local copies, waits for them, and re-layouts: 1.35 us -> none  [per_device(): gain_row = padded(gains.reshape(1, D), DP, 1)]
where the time goes in v2:
time: 122 us
  Pallas kernels  114 us (93%)
  local copies, waits for them, and re-layouts  4.45 us (4%)
  other arithmetic  2.26 us (2%)
    pallas_call x1, Pallas kernels, per_device(): pl.pallas_call(functools.partial(kernel, dims, factor), out_shape=(jax.Sh...  114 us
    unnamed x4, local copies, waits for them, and re-layouts  4.45 us

profile of v2, /device:TPU:0, one launch (start us, length us, event | category | flops | bytes accessed | tf_op | source)
XLA Modules:
  0.0 121.5 jit_solution(10125256662240202161)
XLA Ops:
  0.6 114.2 %shard_map.94 = (bf16[2,1024,512]{2,1,0:T(8,128)(2,1)}, f32[512,1152]{1,0:T(8,128)}, f32[1,4608]{1,0:T(1,128)}) custom-call(bf16[256,4608]{1,0:T(8,128)(2,1)} %bitcast.2, bf16[256,4608]{1,0:T(8,128)(2,1)} %bitcast.3, bf16[2,1024,512]{2,1,0:T(8,128)(2,1)} %att_hbm.1, bf16[512,4608]{1,0:T(8,128)(2,1)} %w_hbm.1, f32[512,1152]{1,0:T(8,128)} %main_hbm.1, ...), custom_call_target="tpu_custom_call" | custom-call | tf_op jit(solution)/shard_map/pallas_call | solution.py:424
  114.8 0.0 copy-start
  114.8 0.9 multiply_reduce_fusion
  115.7 1.3 %add.3 = f32[4608]{0:T(1024)} add(f32[4608]{0:T(1024)} %param.13, f32[4608]{0:T(1024)S(1)} %multiply_reduce_fusion) | non-fusion elementwise | flops 4608 | bytes 55296 | tf_op jit(solution)/shard_map/add | solution.py:456
  117.1 3.0 %copy.12 = bf16[2,1024,512]{2,1,0:T(8,128)(2,1)} copy(bf16[2,1024,512]{2,1,0:T(8,128)(2,1)} %get-tuple-element.12) | data formatting | bytes 4194304
  120.1 0.0 copy-done
  120.1 1.4 %copy.13 = f32[512,1152]{1,0:T(8,128)} copy(f32[512,1152]{1,0:T(8,128)S(1)} %copy-done) | data formatting | bytes 4718592
Async XLA Ops:
  114.8 5.3 %copy-start = (f32[512,1152]{1,0:T(8,128)S(1)}, f32[512,1152]{1,0:T(8,128)}, u32[]{:S(2)}) copy-start(f32[512,1152]{1,0:T(8,128)} %get-tuple-element.13) | copy-start | bytes 7077892
